TPU v7x, 32 devices: a whole 2x2x4 slice. The times are simulated.
32 devices in a mesh: pairs: 2 (over y), gx: 4 (over z), gy: 2 (over x), gz: 2 (over core).
Axes of the slice: x: 2, y: 2, z: 4, core: 2. Of those that a mesh axis runs over, the one named last changes fastest.
Arguments:
- fine_start: float32 [64, 128, 512], P(('pairs', 'gx'), 'gy', 'gz'), parts along dimension 0, may hold values from -1 to 1
- increments: float32 [2, 64, 128, 512], P(None, ('pairs', 'gx'), 'gy', 'gz'), parts along dimension 1, may hold values from -5 to 5
- coarse_start: float32 [32, 64, 256], P(('pairs', 'gx')), parts along dimension 0, may hold values from -1 to 1
Outputs:
- fine_final: float32 [64, 128, 512], P(('pairs', 'gx'), 'gy', 'gz'), parts along dimension 0
- coarse_final: float32 [32, 64, 256], P(('pairs', 'gx')), parts along dimension 0
There are 2 independent parts, one for each index of `pairs`. A program takes and returns all parts, laid end to end along the dimension named above; each array names one. Nothing has to cross between parts.
All inputs are finite; a program needn't handle non-finite values.
Results may differ from a plain program's by a relative error of at most 0.00002.
Values sent between devices are 32-bit elements; how exact they have to be, the bound alone decides.
No kernel may reach another device: no remote copies, remote signals or barrier semaphores. Data moves between devices by JAX's collectives and lax.ppermute only.
A program may use at most 128 MiB of HBM per device.

v0:
```python
import jax
import jax.numpy as jnp
from jax import lax
from jax.sharding import PartitionSpec as P

STEPS = 2
SWEEPS = 2


noise_scale = 0.3
fine_step = 0.2
coarse_step = 0.4
fine_coupling = 1.0
coarse_coupling = 0.5


def with_halo(value, sides, width):
    for axis, dim in sides:
        count, length = (lax.axis_size(axis), value.shape[dim])
        up = [(i, (i + 1) % count) for i in range(count)]
        down = [(j, i) for i, j in up]
        last = lax.slice_in_dim(value, length - width, length, axis=dim)
        first = lax.slice_in_dim(value, 0, width, axis=dim)
        before = lax.ppermute(last, axis, up)
        after = lax.ppermute(first, axis, down)
        value = jnp.concatenate([before, value, after], axis=dim)
    return value


def neighbours(padded):
    beside = padded[2:, 1:-1, 1:-1] + padded[:-2, 1:-1, 1:-1]
    beside = beside + padded[1:-1, 2:, 1:-1] + padded[1:-1, :-2, 1:-1]
    beside = beside + padded[1:-1, 1:-1, 2:] + padded[1:-1, 1:-1, :-2]
    return beside


def trimmed_box(source, margin):
    return source[
        margin : source.shape[0] - margin,
        margin : source.shape[1] - margin,
        margin : source.shape[2] - margin,
    ]


def reaction(state, forcing, step_size):
    return state + step_size * (state - state * state * state) + noise_scale * forcing


def relaxed(source, coupling, extend):
    padded = extend(source, SWEEPS)
    fields = padded
    for sweep_index in range(SWEEPS):
        fields = (trimmed_box(padded, sweep_index + 1) + coupling * neighbours(fields)) / (
            1.0 + 6.0 * coupling
        )
    return fields


def fine_halo(source, width):
    return with_halo(source, (("gx", 0), ("gy", 1), ("gz", 2)), width)


def slab_halo(source, width):
    extended = with_halo(source, (("gx", 0),), width)
    return jnp.pad(extended, ((0, 0), (width, width), (width, width)), mode="wrap")


def assemble(stacked):
    count_y = lax.axis_size("gy")
    count_z = lax.axis_size("gz")
    depth_x, width_y, width_z = (stacked.shape[1], stacked.shape[2], stacked.shape[3])
    blocks = stacked.reshape(count_y, count_z, depth_x, width_y, width_z)
    return blocks.transpose(2, 0, 3, 1, 4).reshape(depth_x, count_y * width_y, count_z * width_z)


def body(fine_start, increments, coarse_start):
    state = fine_start
    for step_index in range(STEPS):
        state = relaxed(
            reaction(state, increments[step_index], fine_step), fine_coupling, fine_halo
        )
    summed = jnp.sum(increments, axis=0)
    half_x, half_y, half_z = (summed.shape[0] // 2, summed.shape[1] // 2, summed.shape[2] // 2)
    partial_value = 0.125 * summed.reshape(half_x, 2, half_y, 2, half_z, 2).sum(axis=(1, 3, 5))
    slab_noise = assemble(lax.all_gather(partial_value[None], ("gy", "gz"), axis=0, tiled=True))
    coarse_final = relaxed(
        reaction(coarse_start, slab_noise, coarse_step), coarse_coupling, slab_halo
    )
    return (state, coarse_final)


def solution(mesh):
    return jax.shard_map(
        body,
        mesh=mesh,
        in_specs=(
            P(("pairs", "gx"), "gy", "gz"),
            P(None, ("pairs", "gx"), "gy", "gz"),
            P(("pairs", "gx"), None, None),
        ),
        out_specs=(P(("pairs", "gx"), "gy", "gz"), P(("pairs", "gx"), None, None)),
        check_vma=False,
    )
```

profile of v0, /device:TPU:0, one launch (start us, length us, event | category | flops | bytes accessed | tf_op | source)
XLA Modules:
  0.0 97.7 jit_solution(14606196234726525269)
XLA Ops:
  0.6 0.0 copy-start
  0.6 1.4 %fusion.15 = f32[8,64,256]{2,1,0:T(8,128)S(1)} fusion(f32[8,64,256]{2,1,0:T(8,128)} %param.3, f32[2,8,64,256]{3,2,1,0:T(8,128)} %param.4), kind=kLoop, calls=%fused_computation.62 | loop fusion | flops 917504 | bytes 1572864 | tf_op jit(solution)/shard_map/add | solution.py:46
  2.1 3.1 %collective-permute-start = (f32[2,64,256]{2,1,0:T(8,128)S(1)}, f32[2,64,256]{2,1,0:T(8,128)S(1)}, u32[]{:S(2)}, u32[]{:S(2)}) collective-permute-start(f32[2,64,256]{2,1,0:T(8,128)S(1)} %get-tuple-element.16), channel_id=1, source_target_pairs={{0,4},{4,8},{8,12},{12,0},{1,5},{5,9},{9,13},{13,1},{2,6},{6,10},{... | collective-permute-start | bytes 393224 | tf_op jit(solution)/shard_map/ppermute | solution.py:24
  5.2 2.1 %collective-permute-start.1 = (f32[2,64,256]{2,1,0:T(8,128)S(1)}, f32[2,64,256]{2,1,0:T(8,128)S(1)}, u32[]{:S(2)}, u32[]{:S(2)}) collective-permute-start(f32[2,64,256]{2,1,0:T(8,128)S(1)} %get-tuple-element.17), channel_id=1, source_target_pairs={{4,0},{8,4},{12,8},{0,12},{5,1},{9,5},{13,9},{1,13},{6,2},{10,6},{... | collective-permute-start | bytes 393224 | tf_op jit(solution)/shard_map/ppermute | solution.py:25
  7.3 0.0 copy-done
  7.3 0.1 reduce_sum.18
  7.4 34.8 %reshape.26 = f32[4,2,32,2,128,2]{5,4,3,2,1,0:T(8,128)} reshape(f32[8,64,256]{2,1,0:T(8,128)S(1)} %reduce_sum.18) | data formatting | bytes 1048576 | tf_op jit(solution)/shard_map/reshape | solution.py:84
  42.2 12.2 %reduce_sum.19 = f32[4,32,128]{2,1,0:T(8,128)S(1)} reduce(f32[4,2,32,2,128,2]{5,4,3,2,1,0:T(8,128)} %reshape.26, f32[]{:T(128)} %constant.6.clone.1), dimensions={1,3,5}, to_apply=%region_1.0 | reduce | flops 114688 | bytes 589828 | tf_op jit(solution)/shard_map/reduce_sum | solution.py:84
  54.5 0.0 copy-start.1
  54.5 6.0 %all-gather = f32[16,32,128]{2,1,0:T(8,128)S(1)} all-gather(f32[4,32,128]{2,1,0:T(8,128)S(1)} %broadcast_multiply_fusion.1), channel_id=2, replica_groups=mesh['pairs'=2,'gx'=4,'gy'=2,'gz'=2] {'gy','gz'}, dimensions={0}, use_global_device_ids=true | all-gather | bytes 327680 | tf_op jit(solution)/shard_map/all_gather | solution.py:85
  60.6 0.2 copy.6
  60.8 0.2 mul.106
  61.0 0.0 copy-done.1
  61.0 0.1 fusion.25
  61.1 0.1 collective-permute-start.12
  61.2 3.8 %collective-permute-start.13 = (f32[2,64,256]{2,1,0:T(8,128)S(1)}, f32[2,64,256]{2,1,0:T(8,128)S(1)}, u32[]{:S(2)}, u32[]{:S(2)}) collective-permute-start(f32[2,64,256]{2,1,0:T(8,128)S(1)} %get-tuple-element.19), channel_id=1, source_target_pairs={{4,0},{8,4},{12,8},{0,12},{5,1},{9,5},{13,9},{1,13},{6,2},{10,6},{... | collective-permute-start | bytes 393224 | tf_op jit(solution)/shard_map/ppermute | solution.py:25
  65.0 0.0 collective-permute-done
  65.0 0.0 collective-permute-done.1
  65.0 1.6 %collective-permute-start.2 = (f32[12,2,256]{2,1,0:T(2,128)S(1)}, f32[12,2,256]{2,1,0:T(2,128)S(1)}, u32[]{:S(2)}, u32[]{:S(2)}) collective-permute-start(f32[12,2,256]{2,1,0:T(2,128)S(1)} %get-tuple-element.8), channel_id=1, source_target_pairs={{0,2},{2,0},{1,3},{3,1},{4,6},{6,4},{5,7},{7,5},{8,10},{10,8},{9,1... | collective-permute-start | bytes 73736 | tf_op jit(solution)/shard_map/ppermute | solution.py:24
  66.6 0.5 collective-permute-start.3
  67.1 2.3 %collective-permute-done.12 = f32[2,64,256]{2,1,0:T(8,128)S(1)} collective-permute-done((f32[2,64,256]{2,1,0:T(8,128)S(1)}, f32[2,64,256]{2,1,0:T(8,128)S(1)}, u32[]{:S(2)}, u32[]{:S(2)}) %collective-permute-start.12) | collective-permute-done | bytes 131104 | tf_op jit(solution)/shard_map/ppermute | solution.py:24
  69.4 0.4 collective-permute-done.13
  69.8 0.1 pad_maximum_fusion.35
  69.9 0.0 collective-permute-done.2
  69.9 0.6 collective-permute-done.3
  70.4 0.1 pad_maximum_fusion.22
  70.5 0.2 fusion.30
  70.7 0.1 collective-permute-start.4
  70.8 0.5 collective-permute-start.5
  71.3 0.1 fusion.31
  71.4 1.1 %collective-permute-done.4 = f32[12,68,2]{2,1,0:T(8,128)S(1)} collective-permute-done((f32[12,68,2]{2,1,0:T(8,128)S(1)}, f32[12,68,2]{2,1,0:T(8,128)S(1)}, u32[]{:S(2)}, u32[]{:S(2)}) %collective-permute-start.4) | collective-permute-done | bytes 6560 | tf_op jit(solution)/shard_map/ppermute | solution.py:24
  72.6 0.6 collective-permute-done.5
  73.2 0.6 pad_maximum_fusion
  73.8 1.9 %fusion.6 = f32[10,66,258]{2,1,0:T(8,128)S(1)} fusion(f32[12,68,2]{2,1,0:T(8,128)S(1)} %collective-permute-done.4, f32[12,2,256]{2,1,0:T(2,128)S(1)} %collective-permute-done.3, f32[12,2,256]{2,1,0:T(2,128)S(1)} %collective-permute-done.2, f32[2,64,256]{2,1,0:T(8,128)S(1)} %collective-permute-done.1, f32[8,64,256]{2,1,0:T(8,128)S(1)} %fusion.15, ...), kind=kLoop, calls=%fused_computation.22 | loop fusion | flops 2894760 | bytes 4935360 | tf_op jit(solution)/shard_map/div | solution.py:53
  75.8 0.8 fusion.18
  76.6 0.6 collective-permute-start.6
  77.1 3.3 %collective-permute-start.7 = (f32[2,64,256]{2,1,0:T(8,128)S(1)}, f32[2,64,256]{2,1,0:T(8,128)S(1)}, u32[]{:S(2)}, u32[]{:S(2)}) collective-permute-start(f32[2,64,256]{2,1,0:T(8,128)S(1)} %get-tuple-element.15), channel_id=1, source_target_pairs={{4,0},{8,4},{12,8},{0,12},{5,1},{9,5},{13,9},{1,13},{6,2},{10,6},{... | collective-permute-start | bytes 393224 | tf_op jit(solution)/shard_map/ppermute | solution.py:25
  80.5 0.4 pad_maximum_fusion.24
  80.9 3.9 %collective-permute-done.6 = f32[2,64,256]{2,1,0:T(8,128)S(1)} collective-permute-done((f32[2,64,256]{2,1,0:T(8,128)S(1)}, f32[2,64,256]{2,1,0:T(8,128)S(1)}, u32[]{:S(2)}, u32[]{:S(2)}) %collective-permute-start.6) | collective-permute-done | bytes 131104 | tf_op jit(solution)/shard_map/ppermute | solution.py:24
  84.9 0.5 collective-permute-done.7
  85.4 1.6 %collective-permute-start.8 = (f32[12,2,256]{2,1,0:T(2,128)S(1)}, f32[12,2,256]{2,1,0:T(2,128)S(1)}, u32[]{:S(2)}, u32[]{:S(2)}) collective-permute-start(f32[12,2,256]{2,1,0:T(2,128)S(1)} %get-tuple-element.6), channel_id=1, source_target_pairs={{0,2},{2,0},{1,3},{3,1},{4,6},{6,4},{5,7},{7,5},{8,10},{10,8},{9,1... | collective-permute-start | bytes 73736 | tf_op jit(solution)/shard_map/ppermute | solution.py:24
  86.9 0.5 collective-permute-start.9
  87.5 1.2 %fusion.11 = f32[6,66,258]{2,1,0:T(8,128)S(1)} fusion(f32[8,68,2]{2,1,0:T(8,128)S(1)} %get-tuple-element.11, f32[8,2,256]{2,1,0:T(2,128)S(1)} %get-tuple-element.13, f32[8,2,256]{2,1,0:T(2,128)S(1)} %get-tuple-element.12, f32[2,64,256]{2,1,0:T(8,128)S(1)} %collective-permute-done.13, f32[4,64,256]{2,1,0:T(8,128)S(1)} %fusion.25, ...), kind=kLoop, calls=%fused_computation.45 | loop fusion | flops 1839024 | bytes 3017792 | tf_op jit(solution)/shard_map/div | solution.py:53
  88.6 0.6 collective-permute-done.8
  89.3 1.5 %collective-permute-done.9 = f32[12,2,256]{2,1,0:T(2,128)S(1)} collective-permute-done((f32[12,2,256]{2,1,0:T(2,128)S(1)}, f32[12,2,256]{2,1,0:T(2,128)S(1)}, u32[]{:S(2)}, u32[]{:S(2)}) %collective-permute-start.9) | collective-permute-done | bytes 24608 | tf_op jit(solution)/shard_map/ppermute | solution.py:25
  90.8 0.1 pad_maximum_fusion.23
  90.9 0.2 fusion.29
  91.1 0.1 collective-permute-start.10
  91.1 0.5 collective-permute-start.11
  91.6 1.1 %fusion.28 = f32[4,64,256]{2,1,0:T(8,128)} fusion(f32[4,64,256]{2,1,0:T(8,128)S(1)} %fusion.25, f32[6,66,258]{2,1,0:T(8,128)S(1)} %fusion.11), kind=kLoop, calls=%fused_computation.87 | loop fusion | flops 524288 | bytes 2097152 | tf_op jit(solution)/shard_map/div | solution.py:53
  92.8 0.2 collective-permute-done.10
  92.9 0.6 collective-permute-done.11
  93.6 0.6 pad_maximum_fusion.1
  94.2 1.9 %fusion.2 = f32[10,66,258]{2,1,0:T(8,128)S(1)} fusion(f32[12,68,2]{2,1,0:T(8,128)S(1)} %collective-permute-done.10, f32[12,2,256]{2,1,0:T(2,128)S(1)} %collective-permute-done.9, f32[12,2,256]{2,1,0:T(2,128)S(1)} %collective-permute-done.8, f32[2,64,256]{2,1,0:T(8,128)S(1)} %collective-permute-done.7, f32[8,64,256]{2,1,0:T(8,128)S(1)} %fusion.18, ...), kind=kLoop, calls=%fused_computation.5 | loop fusion | flops 2894760 | bytes 4935360 | tf_op jit(solution)/shard_map/div | solution.py:53
  96.1 1.6 %fusion.20 = f32[8,64,256]{2,1,0:T(8,128)} fusion(f32[8,64,256]{2,1,0:T(8,128)S(1)} %fusion.18, f32[10,66,258]{2,1,0:T(8,128)S(1)} %fusion.2), kind=kLoop, calls=%fused_computation.68 | loop fusion | flops 917504 | bytes 4194304 | tf_op jit(solution)/shard_map/div | solution.py:53
  (8 shorter events, 0.1 us)
Async XLA Ops:
  0.6 6.7 %copy-start = (f32[2,8,64,256]{3,2,1,0:T(8,128)S(1)}, f32[2,8,64,256]{3,2,1,0:T(8,128)}, u32[]{:S(2)}) copy-start(f32[2,8,64,256]{3,2,1,0:T(8,128)} %param.4) | copy-start | bytes 3145732
  2.1 62.9 %collective-permute-start = (f32[2,64,256]{2,1,0:T(8,128)S(1)}, f32[2,64,256]{2,1,0:T(8,128)S(1)}, u32[]{:S(2)}, u32[]{:S(2)}) collective-permute-start(f32[2,64,256]{2,1,0:T(8,128)S(1)} %get-tuple-element.16), channel_id=1, source_target_pairs={{0,4},{4,8},{8,12},{12,0},{1,5},{5,9},{9,13},{13,1},{2,6},{6,10},{... | collective-permute-start | bytes 393224 | tf_op jit(solution)/shard_map/ppermute | solution.py:24
  5.2 59.8 %collective-permute-start.1 = (f32[2,64,256]{2,1,0:T(8,128)S(1)}, f32[2,64,256]{2,1,0:T(8,128)S(1)}, u32[]{:S(2)}, u32[]{:S(2)}) collective-permute-start(f32[2,64,256]{2,1,0:T(8,128)S(1)} %get-tuple-element.17), channel_id=1, source_target_pairs={{4,0},{8,4},{12,8},{0,12},{5,1},{9,5},{13,9},{1,13},{6,2},{10,6},{... | collective-permute-start | bytes 393224 | tf_op jit(solution)/shard_map/ppermute | solution.py:25
  54.5 6.5 %copy-start.1 = (f32[4,64,256]{2,1,0:T(8,128)S(1)}, f32[4,64,256]{2,1,0:T(8,128)}, u32[]{:S(2)}) copy-start(f32[4,64,256]{2,1,0:T(8,128)} %param.5) | copy-start | bytes 786436
  61.1 8.3 %collective-permute-start.12 = (f32[2,64,256]{2,1,0:T(8,128)S(1)}, f32[2,64,256]{2,1,0:T(8,128)S(1)}, u32[]{:S(2)}, u32[]{:S(2)}) collective-permute-start(f32[2,64,256]{2,1,0:T(8,128)S(1)} %get-tuple-element.18), channel_id=1, source_target_pairs={{0,4},{4,8},{8,12},{12,0},{1,5},{5,9},{9,13},{13,1},{2,6},{6,10},{... | collective-permute-start | bytes 393224 | tf_op jit(solution)/shard_map/ppermute | solution.py:24
  61.2 8.6 %collective-permute-start.13 = (f32[2,64,256]{2,1,0:T(8,128)S(1)}, f32[2,64,256]{2,1,0:T(8,128)S(1)}, u32[]{:S(2)}, u32[]{:S(2)}) collective-permute-start(f32[2,64,256]{2,1,0:T(8,128)S(1)} %get-tuple-element.19), channel_id=1, source_target_pairs={{4,0},{8,4},{12,8},{0,12},{5,1},{9,5},{13,9},{1,13},{6,2},{10,6},{... | collective-permute-start | bytes 393224 | tf_op jit(solution)/shard_map/ppermute | solution.py:25
  65.0 4.9 %collective-permute-start.2 = (f32[12,2,256]{2,1,0:T(2,128)S(1)}, f32[12,2,256]{2,1,0:T(2,128)S(1)}, u32[]{:S(2)}, u32[]{:S(2)}) collective-permute-start(f32[12,2,256]{2,1,0:T(2,128)S(1)} %get-tuple-element.8), channel_id=1, source_target_pairs={{0,2},{2,0},{1,3},{3,1},{4,6},{6,4},{5,7},{7,5},{8,10},{10,8},{9,1... | collective-permute-start | bytes 73736 | tf_op jit(solution)/shard_map/ppermute | solution.py:24
  66.6 3.8 %collective-permute-start.3 = (f32[12,2,256]{2,1,0:T(2,128)S(1)}, f32[12,2,256]{2,1,0:T(2,128)S(1)}, u32[]{:S(2)}, u32[]{:S(2)}) collective-permute-start(f32[12,2,256]{2,1,0:T(2,128)S(1)} %get-tuple-element.9), channel_id=1, source_target_pairs={{2,0},{0,2},{3,1},{1,3},{6,4},{4,6},{7,5},{5,7},{10,8},{8,10},{11,... | collective-permute-start | bytes 73736 | tf_op jit(solution)/shard_map/ppermute | solution.py:25
  70.7 1.9 %collective-permute-start.4 = (f32[12,68,2]{2,1,0:T(8,128)S(1)}, f32[12,68,2]{2,1,0:T(8,128)S(1)}, u32[]{:S(2)}, u32[]{:S(2)}) collective-permute-start(f32[12,68,2]{2,1,0:T(8,128)S(1)} %get-tuple-element.5), channel_id=1, source_target_pairs={{0,1},{1,0},{2,3},{3,2},{4,5},{5,4},{6,7},{7,6},{8,9},{9,8},{10,11... | collective-permute-start | bytes 19592 | tf_op jit(solution)/shard_map/ppermute | solution.py:24
  70.8 2.4 %collective-permute-start.5 = (f32[12,68,2]{2,1,0:T(8,128)S(1)}, f32[12,68,2]{2,1,0:T(8,128)S(1)}, u32[]{:S(2)}, u32[]{:S(2)}) collective-permute-start(f32[12,68,2]{2,1,0:T(8,128)S(1)} %get-tuple-element.4), channel_id=1, source_target_pairs={{1,0},{0,1},{3,2},{2,3},{5,4},{4,5},{7,6},{6,7},{9,8},{8,9},{11,10... | collective-permute-start | bytes 19592 | tf_op jit(solution)/shard_map/ppermute | solution.py:25
  76.6 8.3 %collective-permute-start.6 = (f32[2,64,256]{2,1,0:T(8,128)S(1)}, f32[2,64,256]{2,1,0:T(8,128)S(1)}, u32[]{:S(2)}, u32[]{:S(2)}) collective-permute-start(f32[2,64,256]{2,1,0:T(8,128)S(1)} %get-tuple-element.14), channel_id=1, source_target_pairs={{0,4},{4,8},{8,12},{12,0},{1,5},{5,9},{9,13},{13,1},{2,6},{6,10},{... | collective-permute-start | bytes 393224 | tf_op jit(solution)/shard_map/ppermute | solution.py:24
  77.1 8.2 %collective-permute-start.7 = (f32[2,64,256]{2,1,0:T(8,128)S(1)}, f32[2,64,256]{2,1,0:T(8,128)S(1)}, u32[]{:S(2)}, u32[]{:S(2)}) collective-permute-start(f32[2,64,256]{2,1,0:T(8,128)S(1)} %get-tuple-element.15), channel_id=1, source_target_pairs={{4,0},{8,4},{12,8},{0,12},{5,1},{9,5},{13,9},{1,13},{6,2},{10,6},{... | collective-permute-start | bytes 393224 | tf_op jit(solution)/shard_map/ppermute | solution.py:25
  85.4 3.9 %collective-permute-start.8 = (f32[12,2,256]{2,1,0:T(2,128)S(1)}, f32[12,2,256]{2,1,0:T(2,128)S(1)}, u32[]{:S(2)}, u32[]{:S(2)}) collective-permute-start(f32[12,2,256]{2,1,0:T(2,128)S(1)} %get-tuple-element.6), channel_id=1, source_target_pairs={{0,2},{2,0},{1,3},{3,1},{4,6},{6,4},{5,7},{7,5},{8,10},{10,8},{9,1... | collective-permute-start | bytes 73736 | tf_op jit(solution)/shard_map/ppermute | solution.py:24
  86.9 3.8 %collective-permute-start.9 = (f32[12,2,256]{2,1,0:T(2,128)S(1)}, f32[12,2,256]{2,1,0:T(2,128)S(1)}, u32[]{:S(2)}, u32[]{:S(2)}) collective-permute-start(f32[12,2,256]{2,1,0:T(2,128)S(1)} %get-tuple-element.7), channel_id=1, source_target_pairs={{2,0},{0,2},{3,1},{1,3},{6,4},{4,6},{7,5},{5,7},{10,8},{8,10},{11,... | collective-permute-start | bytes 73736 | tf_op jit(solution)/shard_map/ppermute | solution.py:25
  91.1 1.9 %collective-permute-start.10 = (f32[12,68,2]{2,1,0:T(8,128)S(1)}, f32[12,68,2]{2,1,0:T(8,128)S(1)}, u32[]{:S(2)}, u32[]{:S(2)}) collective-permute-start(f32[12,68,2]{2,1,0:T(8,128)S(1)} %get-tuple-element.3), channel_id=1, source_target_pairs={{0,1},{1,0},{2,3},{3,2},{4,5},{5,4},{6,7},{7,6},{8,9},{9,8},{10,11... | collective-permute-start | bytes 19592 | tf_op jit(solution)/shard_map/ppermute | solution.py:24
  91.1 2.4 %collective-permute-start.11 = (f32[12,68,2]{2,1,0:T(8,128)S(1)}, f32[12,68,2]{2,1,0:T(8,128)S(1)}, u32[]{:S(2)}, u32[]{:S(2)}) collective-permute-start(f32[12,68,2]{2,1,0:T(8,128)S(1)} %get-tuple-element.2), channel_id=1, source_target_pairs={{1,0},{0,1},{3,2},{2,3},{5,4},{4,5},{7,6},{6,7},{9,8},{8,9},{11,10... | collective-permute-start | bytes 19592 | tf_op jit(solution)/shard_map/ppermute | solution.py:25
where the time goes:
time: 97.9 us; the launch traced here: 97.7 us
  local copies, waits for them, and re-layouts  35.8 us (37%)
  other arithmetic  24.4 us (25%)
  starting transfers between devices  18.3 us (19%)
  waiting for transfers between devices  12.4 us (13%)
  blocking collectives  6.03 us (6%)
    reshape x1, local copies, waits for them, and re-layouts, body(): summed.reshape(half_x, 2, half_y, 2, half_z, 2).sum(axis=(1, 3, 5))  34.8 us
    reduce_sum x1, other arithmetic, body(): summed.reshape(half_x, 2, half_y, 2, half_z, 2).sum(axis=(1, 3, 5))  12.2 us
    ppermute x7, starting transfers between devices, with_halo(): after = lax.ppermute(first, axis, down)  11.2 us
    ppermute x7, waiting for transfers between devices, with_halo(): before = lax.ppermute(last, axis, up)  8.15 us
    div x5, other arithmetic, relaxed(): (trimmed_box(padded, sweep_index + 1) + coupling * neighbours(fields)) /...  7.7 us
    ppermute x7, starting transfers between devices, with_halo(): before = lax.ppermute(last, axis, up)  7.04 us
    all_gather x1, blocking collectives, body(): lax.all_gather(partial_value[None], ('gy', 'gz'), axis=0, tiled=True)  6.03 us
    ppermute x7, waiting for transfers between devices, with_halo(): after = lax.ppermute(first, axis, down)  4.23 us
  transfers between devices with their start and end apart: 14, of which 11 were waited for; matrix products, arithmetic and copies ran while one was open for 52% of the time, Pallas kernels for 0%

commit v1 on v0

--- a/solution.py
+++ b/solution.py
@@ -73,15 +73,24 @@
     return blocks.transpose(2, 0, 3, 1, 4).reshape(depth_x, count_y * width_y, count_z * width_z)
 
 
+def pair_sum(length):
+    fine = lax.broadcasted_iota(jnp.int32, (length, length // 2), 0)
+    coarse = lax.broadcasted_iota(jnp.int32, (length, length // 2), 1)
+    return (fine // 2 == coarse).astype(jnp.float32)
+
+
 def body(fine_start, increments, coarse_start):
     state = fine_start
     for step_index in range(STEPS):
         state = relaxed(
             reaction(state, increments[step_index], fine_step), fine_coupling, fine_halo
         )
-    summed = jnp.sum(increments, axis=0)
-    half_x, half_y, half_z = (summed.shape[0] // 2, summed.shape[1] // 2, summed.shape[2] // 2)
-    partial_value = 0.125 * summed.reshape(half_x, 2, half_y, 2, half_z, 2).sum(axis=(1, 3, 5))
+    depth_x, width_y, width_z = increments.shape[1:]
+    layers = increments.reshape(STEPS, depth_x // 2, 2, width_y, width_z).sum(axis=(0, 2))
+    rows = lax.dot_general(
+        layers.reshape(-1, width_z), pair_sum(width_z), (((1,), (0,)), ((), ())), precision="highest"
+    ).reshape(depth_x // 2, width_y, width_z // 2)
+    partial_value = 0.125 * jnp.einsum("ab,xbz->xaz", pair_sum(width_y).T, rows, precision="highest")
     slab_noise = assemble(lax.all_gather(partial_value[None], ("gy", "gz"), axis=0, tiled=True))
     coarse_final = relaxed(
         reaction(coarse_start, slab_noise, coarse_step), coarse_coupling, slab_halo

time: 97.9 us -> 52.8 us (0.54)
  local copies, waits for them, and re-layouts: 35.8 us -> 0.99 us
  other arithmetic: 24.4 us -> 12.2 us
  waiting for transfers between devices: 12.4 us -> 15.9 us
  starting transfers between devices: 18.3 us -> 16.4 us
    reshape x1 -> x0, local copies, waits for them, and re-layouts: 34.8 us -> none  [body(): summed.reshape(half_x, 2, half_y, 2, half_z, 2).sum(axis=(1, 3, 5))]
    reduce_sum x2, other arithmetic: 12.3 us -> 0.14 us  [body(): increments.reshape(STEPS, depth_x // 2, 2, width_y, width_z)]
    ppermute x7, starting transfers between devices: 7.04 us -> 1.88 us  [with_halo(): before = lax.ppermute(last, axis, up)]
    ppermute x7, starting transfers between devices: 11.2 us -> 14.5 us  [with_halo(): after = lax.ppermute(first, axis, down)]
    ppermute x7, waiting for transfers between devices: 4.23 us -> 6.98 us  [with_halo(): after = lax.ppermute(first, axis, down)]
  transfers between devices with their start and end apart: 14 -> 14, of which waited for: 11 -> 10; matrix products, arithmetic and copies ran while one was open for 52% -> 8% of each run, Pallas kernels for 0% -> 0%
where the time goes in v1:
time: 52.8 us; the launch traced here: 52.7 us
  starting transfers between devices  16.4 us (31%)
  waiting for transfers between devices  15.9 us (30%)
  other arithmetic  12.2 us (23%)
  blocking collectives  5.78 us (11%)
  local copies, waits for them, and re-layouts  0.99 us (2%)
  between operations  0.88 us (2%)
  matrix products  0.59 us (1%)
    ppermute x7, starting transfers between devices, with_halo(): after = lax.ppermute(first, axis, down)  14.5 us
    ppermute x7, waiting for transfers between devices, with_halo(): before = lax.ppermute(last, axis, up)  8.9 us
    div x5, other arithmetic, relaxed(): (trimmed_box(padded, sweep_index + 1) + coupling * neighbours(fields)) /...  7.7 us
    ppermute x7, waiting for transfers between devices, with_halo(): after = lax.ppermute(first, axis, down)  6.98 us
    all_gather x1, blocking collectives, body(): lax.all_gather(partial_value[None], ('gy', 'gz'), axis=0, tiled=True)  5.78 us
    add x3, other arithmetic, reaction(): state + step_size * (state - state * state * state) + noise_scale * forcing  2.24 us
    ppermute x7, starting transfers between devices, with_halo(): before = lax.ppermute(last, axis, up)  1.88 us
    concatenate x4, other arithmetic, with_halo(): value = jnp.concatenate([before, value, after], axis=dim)  1.5 us
  transfers between devices with their start and end apart: 14, of which 10 were waited for; matrix products, arithmetic and copies ran while one was open for 8% of the time, Pallas kernels for 0%

profile of v1, /device:TPU:0, one launch (start us, length us, event | category | flops | bytes accessed | tf_op | source)
XLA Modules:
  0.0 52.7 jit_solution(18117565459491514099)
XLA Ops:
  0.6 0.0 copy-start
  0.6 1.4 %fusion.16 = f32[8,64,256]{2,1,0:T(8,128)S(1)} fusion(f32[8,64,256]{2,1,0:T(8,128)} %param.3, f32[2,8,64,256]{3,2,1,0:T(8,128)} %param.4), kind=kLoop, calls=%fused_computation.64 | loop fusion | flops 917504 | bytes 1572864 | tf_op jit(solution)/shard_map/add | solution.py:46
  2.1 5.1 %collective-permute-start.1 = (f32[2,64,256]{2,1,0:T(8,128)S(1)}, f32[2,64,256]{2,1,0:T(8,128)S(1)}, u32[]{:S(2)}, u32[]{:S(2)}) collective-permute-start(f32[2,64,256]{2,1,0:T(8,128)S(1)} %get-tuple-element.17), channel_id=1, source_target_pairs={{4,0},{8,4},{12,8},{0,12},{5,1},{9,5},{13,9},{1,13},{6,2},{10,6},{... | collective-permute-start | bytes 393224 | tf_op jit(solution)/shard_map/ppermute | solution.py:25
  7.2 0.0 collective-permute-start
  7.3 0.0 copy-done
  7.3 0.1 reduce_sum.10
  7.4 0.4 fusion.31
  7.8 0.0 copy-start.1
  7.8 0.2 fusion
  8.0 5.8 %all-gather = f32[16,32,128]{2,1,0:T(8,128)S(1)} all-gather(f32[4,32,128]{2,1,0:T(8,128)S(1)} %fusion), channel_id=2, replica_groups=mesh['pairs'=2,'gx'=4,'gy'=2,'gz'=2] {'gy','gz'}, dimensions={0}, use_global_device_ids=true | all-gather | bytes 327680 | tf_op jit(solution)/shard_map/all_gather | solution.py:94
  13.8 0.2 copy.7
  14.1 0.2 mul.99
  14.3 0.0 copy-done.1
  14.3 0.1 fusion.26
  14.4 3.9 %collective-permute-start.13 = (f32[2,64,256]{2,1,0:T(8,128)S(1)}, f32[2,64,256]{2,1,0:T(8,128)S(1)}, u32[]{:S(2)}, u32[]{:S(2)}) collective-permute-start(f32[2,64,256]{2,1,0:T(8,128)S(1)} %get-tuple-element.19), channel_id=1, source_target_pairs={{4,0},{8,4},{12,8},{0,12},{5,1},{9,5},{13,9},{1,13},{6,2},{10,6},{... | collective-permute-start | bytes 393224 | tf_op jit(solution)/shard_map/ppermute | solution.py:25
  18.2 0.0 collective-permute-start.12
  18.3 0.0 collective-permute-done.1
  18.3 0.0 collective-permute-done
  18.3 1.6 %collective-permute-start.3 = (f32[12,2,256]{2,1,0:T(2,128)S(1)}, f32[12,2,256]{2,1,0:T(2,128)S(1)}, u32[]{:S(2)}, u32[]{:S(2)}) collective-permute-start(f32[12,2,256]{2,1,0:T(2,128)S(1)} %get-tuple-element.9), channel_id=1, source_target_pairs={{2,0},{0,2},{3,1},{1,3},{6,4},{4,6},{7,5},{5,7},{10,8},{8,10},{11,... | collective-permute-start | bytes 73736 | tf_op jit(solution)/shard_map/ppermute | solution.py:25
  19.8 0.5 %collective-permute-start.2 = (f32[12,2,256]{2,1,0:T(2,128)S(1)}, f32[12,2,256]{2,1,0:T(2,128)S(1)}, u32[]{:S(2)}, u32[]{:S(2)}) collective-permute-start(f32[12,2,256]{2,1,0:T(2,128)S(1)} %get-tuple-element.8), channel_id=1, source_target_pairs={{0,2},{2,0},{1,3},{3,1},{4,6},{6,4},{5,7},{7,5},{8,10},{10,8},{9,1... | collective-permute-start | bytes 73736 | tf_op jit(solution)/shard_map/ppermute | solution.py:24
  20.4 1.8 %collective-permute-done.13 = f32[2,64,256]{2,1,0:T(8,128)S(1)} collective-permute-done((f32[2,64,256]{2,1,0:T(8,128)S(1)}, f32[2,64,256]{2,1,0:T(8,128)S(1)}, u32[]{:S(2)}, u32[]{:S(2)}) %collective-permute-start.13) | collective-permute-done | bytes 131104 | tf_op jit(solution)/shard_map/ppermute | solution.py:25
  22.1 3.4 %collective-permute-done.12 = f32[2,64,256]{2,1,0:T(8,128)S(1)} collective-permute-done((f32[2,64,256]{2,1,0:T(8,128)S(1)}, f32[2,64,256]{2,1,0:T(8,128)S(1)}, u32[]{:S(2)}, u32[]{:S(2)}) %collective-permute-start.12) | collective-permute-done | bytes 131104 | tf_op jit(solution)/shard_map/ppermute | solution.py:24
  25.5 0.1 pad_maximum_fusion.35
  25.6 0.0 collective-permute-done.3
  25.6 0.0 collective-permute-done.2
  25.6 0.1 pad_maximum_fusion.22
  25.7 0.2 fusion.42
  25.9 0.1 collective-permute-start.4
  26.0 0.5 collective-permute-start.5
  26.5 0.1 fusion.43
  26.6 1.1 %collective-permute-done.4 = f32[12,68,2]{2,1,0:T(8,128)S(1)} collective-permute-done((f32[12,68,2]{2,1,0:T(8,128)S(1)}, f32[12,68,2]{2,1,0:T(8,128)S(1)}, u32[]{:S(2)}, u32[]{:S(2)}) %collective-permute-start.4) | collective-permute-done | bytes 6560 | tf_op jit(solution)/shard_map/ppermute | solution.py:24
  27.8 0.6 %collective-permute-done.5 = f32[12,68,2]{2,1,0:T(8,128)S(1)} collective-permute-done((f32[12,68,2]{2,1,0:T(8,128)S(1)}, f32[12,68,2]{2,1,0:T(8,128)S(1)}, u32[]{:S(2)}, u32[]{:S(2)}) %collective-permute-start.5) | collective-permute-done | bytes 6560 | tf_op jit(solution)/shard_map/ppermute | solution.py:25
  28.4 0.6 %pad_maximum_fusion = f32[12,68,260]{2,1,0:T(8,128)S(1)} fusion(f32[12,68,2]{2,1,0:T(8,128)S(1)} %collective-permute-done.5, f32[12,2,256]{2,1,0:T(2,128)S(1)} %collective-permute-done.3, f32[2,64,256]{2,1,0:T(8,128)S(1)} %collective-permute-done.1, f32[8,64,256]{2,1,0:T(8,128)S(1)} %fusion.16, f32[2,64,256]{2,1,0:T(8,128)S(1)} %collective-permute-done, ...), kind=kLoop, calls=%fused_computation | loop fusion | flops 1272960 | bytes 1697280 | tf_op jit(solution)/shard_map/concatenate | solution.py:26
  29.1 1.9 %fusion.7 = f32[10,66,258]{2,1,0:T(8,128)S(1)} fusion(f32[12,68,2]{2,1,0:T(8,128)S(1)} %collective-permute-done.4, f32[12,2,256]{2,1,0:T(2,128)S(1)} %collective-permute-done.3, f32[12,2,256]{2,1,0:T(2,128)S(1)} %collective-permute-done.2, f32[2,64,256]{2,1,0:T(8,128)S(1)} %collective-permute-done.1, f32[8,64,256]{2,1,0:T(8,128)S(1)} %fusion.16, ...), kind=kLoop, calls=%fused_computation.24 | loop fusion | flops 2894760 | bytes 4935360 | tf_op jit(solution)/shard_map/div | solution.py:53
  31.0 0.8 %fusion.19 = f32[8,64,256]{2,1,0:T(8,128)S(1)} fusion(f32[8,64,256]{2,1,0:T(8,128)S(1)} %fusion.16, f32[10,66,258]{2,1,0:T(8,128)S(1)} %fusion.7, f32[2,8,64,256]{3,2,1,0:T(8,128)S(1)} %copy-done), kind=kLoop, calls=%fused_computation.67 | loop fusion | flops 1835008 | bytes 4718592 | tf_op jit(solution)/shard_map/add | solution.py:46
  31.8 1.9 %collective-permute-start.7 = (f32[2,64,256]{2,1,0:T(8,128)S(1)}, f32[2,64,256]{2,1,0:T(8,128)S(1)}, u32[]{:S(2)}, u32[]{:S(2)}) collective-permute-start(f32[2,64,256]{2,1,0:T(8,128)S(1)} %get-tuple-element.15), channel_id=1, source_target_pairs={{4,0},{8,4},{12,8},{0,12},{5,1},{9,5},{13,9},{1,13},{6,2},{10,6},{... | collective-permute-start | bytes 393224 | tf_op jit(solution)/shard_map/ppermute | solution.py:25
  33.7 0.2 collective-permute-start.6
  33.9 0.4 pad_maximum_fusion.24
  34.3 3.3 %collective-permute-done.7 = f32[2,64,256]{2,1,0:T(8,128)S(1)} collective-permute-done((f32[2,64,256]{2,1,0:T(8,128)S(1)}, f32[2,64,256]{2,1,0:T(8,128)S(1)}, u32[]{:S(2)}, u32[]{:S(2)}) %collective-permute-start.7) | collective-permute-done | bytes 131104 | tf_op jit(solution)/shard_map/ppermute | solution.py:25
  37.6 3.2 %collective-permute-done.6 = f32[2,64,256]{2,1,0:T(8,128)S(1)} collective-permute-done((f32[2,64,256]{2,1,0:T(8,128)S(1)}, f32[2,64,256]{2,1,0:T(8,128)S(1)}, u32[]{:S(2)}, u32[]{:S(2)}) %collective-permute-start.6) | collective-permute-done | bytes 131104 | tf_op jit(solution)/shard_map/ppermute | solution.py:24
  40.9 1.1 %collective-permute-start.9 = (f32[12,2,256]{2,1,0:T(2,128)S(1)}, f32[12,2,256]{2,1,0:T(2,128)S(1)}, u32[]{:S(2)}, u32[]{:S(2)}) collective-permute-start(f32[12,2,256]{2,1,0:T(2,128)S(1)} %get-tuple-element.7), channel_id=1, source_target_pairs={{2,0},{0,2},{3,1},{1,3},{6,4},{4,6},{7,5},{5,7},{10,8},{8,10},{11,... | collective-permute-start | bytes 73736 | tf_op jit(solution)/shard_map/ppermute | solution.py:25
  41.9 1.0 %collective-permute-start.8 = (f32[12,2,256]{2,1,0:T(2,128)S(1)}, f32[12,2,256]{2,1,0:T(2,128)S(1)}, u32[]{:S(2)}, u32[]{:S(2)}) collective-permute-start(f32[12,2,256]{2,1,0:T(2,128)S(1)} %get-tuple-element.6), channel_id=1, source_target_pairs={{0,2},{2,0},{1,3},{3,1},{4,6},{6,4},{5,7},{7,5},{8,10},{10,8},{9,1... | collective-permute-start | bytes 73736 | tf_op jit(solution)/shard_map/ppermute | solution.py:24
  43.0 1.2 %fusion.12 = f32[6,66,258]{2,1,0:T(8,128)S(1)} fusion(f32[8,68,2]{2,1,0:T(8,128)S(1)} %get-tuple-element.11, f32[8,2,256]{2,1,0:T(2,128)S(1)} %get-tuple-element.13, f32[8,2,256]{2,1,0:T(2,128)S(1)} %get-tuple-element.12, f32[2,64,256]{2,1,0:T(8,128)S(1)} %collective-permute-done.13, f32[4,64,256]{2,1,0:T(8,128)S(1)} %fusion.26, ...), kind=kLoop, calls=%fused_computation.47 | loop fusion | flops 1839024 | bytes 3017792 | tf_op jit(solution)/shard_map/div | solution.py:53
  44.2 0.6 %collective-permute-done.9 = f32[12,2,256]{2,1,0:T(2,128)S(1)} collective-permute-done((f32[12,2,256]{2,1,0:T(2,128)S(1)}, f32[12,2,256]{2,1,0:T(2,128)S(1)}, u32[]{:S(2)}, u32[]{:S(2)}) %collective-permute-start.9) | collective-permute-done | bytes 24608 | tf_op jit(solution)/shard_map/ppermute | solution.py:25
  44.8 1.0 %collective-permute-done.8 = f32[12,2,256]{2,1,0:T(2,128)S(1)} collective-permute-done((f32[12,2,256]{2,1,0:T(2,128)S(1)}, f32[12,2,256]{2,1,0:T(2,128)S(1)}, u32[]{:S(2)}, u32[]{:S(2)}) %collective-permute-start.8) | collective-permute-done | bytes 24608 | tf_op jit(solution)/shard_map/ppermute | solution.py:24
  45.8 0.1 pad_maximum_fusion.23
  45.9 0.2 fusion.41
  46.1 0.1 collective-permute-start.10
  46.1 0.5 collective-permute-start.11
  46.6 1.1 %fusion.29 = f32[4,64,256]{2,1,0:T(8,128)} fusion(f32[4,64,256]{2,1,0:T(8,128)S(1)} %fusion.26, f32[6,66,258]{2,1,0:T(8,128)S(1)} %fusion.12), kind=kLoop, calls=%fused_computation.90 | loop fusion | flops 524288 | bytes 2097152 | tf_op jit(solution)/shard_map/div | solution.py:53
  47.8 0.2 collective-permute-done.10
  47.9 0.6 %collective-permute-done.11 = f32[12,68,2]{2,1,0:T(8,128)S(1)} collective-permute-done((f32[12,68,2]{2,1,0:T(8,128)S(1)}, f32[12,68,2]{2,1,0:T(8,128)S(1)}, u32[]{:S(2)}, u32[]{:S(2)}) %collective-permute-start.11) | collective-permute-done | bytes 6560 | tf_op jit(solution)/shard_map/ppermute | solution.py:25
  48.6 0.6 %pad_maximum_fusion.1 = f32[12,68,260]{2,1,0:T(8,128)S(1)} fusion(f32[12,68,2]{2,1,0:T(8,128)S(1)} %collective-permute-done.11, f32[12,2,256]{2,1,0:T(2,128)S(1)} %collective-permute-done.9, f32[2,64,256]{2,1,0:T(8,128)S(1)} %collective-permute-done.7, f32[8,64,256]{2,1,0:T(8,128)S(1)} %fusion.19, f32[2,64,256]{2,1,0:T(8,128)S(1)} %collective-permute-done.6, ...), kind=kLoop, calls=%fused_computation.1 | loop fusion | flops 1272960 | bytes 1697280 | tf_op jit(solution)/shard_map/concatenate | solution.py:26
  49.2 1.9 %fusion.3 = f32[10,66,258]{2,1,0:T(8,128)S(1)} fusion(f32[12,68,2]{2,1,0:T(8,128)S(1)} %collective-permute-done.10, f32[12,2,256]{2,1,0:T(2,128)S(1)} %collective-permute-done.9, f32[12,2,256]{2,1,0:T(2,128)S(1)} %collective-permute-done.8, f32[2,64,256]{2,1,0:T(8,128)S(1)} %collective-permute-done.7, f32[8,64,256]{2,1,0:T(8,128)S(1)} %fusion.19, ...), kind=kLoop, calls=%fused_computation.7 | loop fusion | flops 2894760 | bytes 4935360 | tf_op jit(solution)/shard_map/div | solution.py:53
  51.1 1.6 %fusion.21 = f32[8,64,256]{2,1,0:T(8,128)} fusion(f32[8,64,256]{2,1,0:T(8,128)S(1)} %fusion.19, f32[10,66,258]{2,1,0:T(8,128)S(1)} %fusion.3), kind=kLoop, calls=%fused_computation.70 | loop fusion | flops 917504 | bytes 4194304 | tf_op jit(solution)/shard_map/div | solution.py:53
  (12 shorter events, 0.2 us)
Async XLA Ops:
  0.6 6.6 %copy-start = (f32[2,8,64,256]{3,2,1,0:T(8,128)S(1)}, f32[2,8,64,256]{3,2,1,0:T(8,128)}, u32[]{:S(2)}) copy-start(f32[2,8,64,256]{3,2,1,0:T(8,128)} %param.4) | copy-start | bytes 3145732
  2.1 16.2 %collective-permute-start.1 = (f32[2,64,256]{2,1,0:T(8,128)S(1)}, f32[2,64,256]{2,1,0:T(8,128)S(1)}, u32[]{:S(2)}, u32[]{:S(2)}) collective-permute-start(f32[2,64,256]{2,1,0:T(8,128)S(1)} %get-tuple-element.17), channel_id=1, source_target_pairs={{4,0},{8,4},{12,8},{0,12},{5,1},{9,5},{13,9},{1,13},{6,2},{10,6},{... | collective-permute-start | bytes 393224 | tf_op jit(solution)/shard_map/ppermute | solution.py:25
  7.2 11.0 %collective-permute-start = (f32[2,64,256]{2,1,0:T(8,128)S(1)}, f32[2,64,256]{2,1,0:T(8,128)S(1)}, u32[]{:S(2)}, u32[]{:S(2)}) collective-permute-start(f32[2,64,256]{2,1,0:T(8,128)S(1)} %get-tuple-element.16), channel_id=1, source_target_pairs={{0,4},{4,8},{8,12},{12,0},{1,5},{5,9},{9,13},{13,1},{2,6},{6,10},{... | collective-permute-start | bytes 393224 | tf_op jit(solution)/shard_map/ppermute | solution.py:24
  7.8 6.4 %copy-start.1 = (f32[4,64,256]{2,1,0:T(8,128)S(1)}, f32[4,64,256]{2,1,0:T(8,128)}, u32[]{:S(2)}) copy-start(f32[4,64,256]{2,1,0:T(8,128)} %param.5) | copy-start | bytes 786436
  14.4 7.8 %collective-permute-start.13 = (f32[2,64,256]{2,1,0:T(8,128)S(1)}, f32[2,64,256]{2,1,0:T(8,128)S(1)}, u32[]{:S(2)}, u32[]{:S(2)}) collective-permute-start(f32[2,64,256]{2,1,0:T(8,128)S(1)} %get-tuple-element.19), channel_id=1, source_target_pairs={{4,0},{8,4},{12,8},{0,12},{5,1},{9,5},{13,9},{1,13},{6,2},{10,6},{... | collective-permute-start | bytes 393224 | tf_op jit(solution)/shard_map/ppermute | solution.py:25
  18.2 7.3 %collective-permute-start.12 = (f32[2,64,256]{2,1,0:T(8,128)S(1)}, f32[2,64,256]{2,1,0:T(8,128)S(1)}, u32[]{:S(2)}, u32[]{:S(2)}) collective-permute-start(f32[2,64,256]{2,1,0:T(8,128)S(1)} %get-tuple-element.18), channel_id=1, source_target_pairs={{0,4},{4,8},{8,12},{12,0},{1,5},{5,9},{9,13},{13,1},{2,6},{6,10},{... | collective-permute-start | bytes 393224 | tf_op jit(solution)/shard_map/ppermute | solution.py:24
  18.3 7.3 %collective-permute-start.3 = (f32[12,2,256]{2,1,0:T(2,128)S(1)}, f32[12,2,256]{2,1,0:T(2,128)S(1)}, u32[]{:S(2)}, u32[]{:S(2)}) collective-permute-start(f32[12,2,256]{2,1,0:T(2,128)S(1)} %get-tuple-element.9), channel_id=1, source_target_pairs={{2,0},{0,2},{3,1},{1,3},{6,4},{4,6},{7,5},{5,7},{10,8},{8,10},{11,... | collective-permute-start | bytes 73736 | tf_op jit(solution)/shard_map/ppermute | solution.py:25
  19.8 5.8 %collective-permute-start.2 = (f32[12,2,256]{2,1,0:T(2,128)S(1)}, f32[12,2,256]{2,1,0:T(2,128)S(1)}, u32[]{:S(2)}, u32[]{:S(2)}) collective-permute-start(f32[12,2,256]{2,1,0:T(2,128)S(1)} %get-tuple-element.8), channel_id=1, source_target_pairs={{0,2},{2,0},{1,3},{3,1},{4,6},{6,4},{5,7},{7,5},{8,10},{10,8},{9,1... | collective-permute-start | bytes 73736 | tf_op jit(solution)/shard_map/ppermute | solution.py:24
  25.9 1.9 %collective-permute-start.4 = (f32[12,68,2]{2,1,0:T(8,128)S(1)}, f32[12,68,2]{2,1,0:T(8,128)S(1)}, u32[]{:S(2)}, u32[]{:S(2)}) collective-permute-start(f32[12,68,2]{2,1,0:T(8,128)S(1)} %get-tuple-element.5), channel_id=1, source_target_pairs={{0,1},{1,0},{2,3},{3,2},{4,5},{5,4},{6,7},{7,6},{8,9},{9,8},{10,11... | collective-permute-start | bytes 19592 | tf_op jit(solution)/shard_map/ppermute | solution.py:24
  26.0 2.4 %collective-permute-start.5 = (f32[12,68,2]{2,1,0:T(8,128)S(1)}, f32[12,68,2]{2,1,0:T(8,128)S(1)}, u32[]{:S(2)}, u32[]{:S(2)}) collective-permute-start(f32[12,68,2]{2,1,0:T(8,128)S(1)} %get-tuple-element.4), channel_id=1, source_target_pairs={{1,0},{0,1},{3,2},{2,3},{5,4},{4,5},{7,6},{6,7},{9,8},{8,9},{11,10... | collective-permute-start | bytes 19592 | tf_op jit(solution)/shard_map/ppermute | solution.py:25
  31.8 5.8 %collective-permute-start.7 = (f32[2,64,256]{2,1,0:T(8,128)S(1)}, f32[2,64,256]{2,1,0:T(8,128)S(1)}, u32[]{:S(2)}, u32[]{:S(2)}) collective-permute-start(f32[2,64,256]{2,1,0:T(8,128)S(1)} %get-tuple-element.15), channel_id=1, source_target_pairs={{4,0},{8,4},{12,8},{0,12},{5,1},{9,5},{13,9},{1,13},{6,2},{10,6},{... | collective-permute-start | bytes 393224 | tf_op jit(solution)/shard_map/ppermute | solution.py:25
  33.7 7.2 %collective-permute-start.6 = (f32[2,64,256]{2,1,0:T(8,128)S(1)}, f32[2,64,256]{2,1,0:T(8,128)S(1)}, u32[]{:S(2)}, u32[]{:S(2)}) collective-permute-start(f32[2,64,256]{2,1,0:T(8,128)S(1)} %get-tuple-element.14), channel_id=1, source_target_pairs={{0,4},{4,8},{8,12},{12,0},{1,5},{5,9},{9,13},{13,1},{2,6},{6,10},{... | collective-permute-start | bytes 393224 | tf_op jit(solution)/shard_map/ppermute | solution.py:24
  40.9 3.9 %collective-permute-start.9 = (f32[12,2,256]{2,1,0:T(2,128)S(1)}, f32[12,2,256]{2,1,0:T(2,128)S(1)}, u32[]{:S(2)}, u32[]{:S(2)}) collective-permute-start(f32[12,2,256]{2,1,0:T(2,128)S(1)} %get-tuple-element.7), channel_id=1, source_target_pairs={{2,0},{0,2},{3,1},{1,3},{6,4},{4,6},{7,5},{5,7},{10,8},{8,10},{11,... | collective-permute-start | bytes 73736 | tf_op jit(solution)/shard_map/ppermute | solution.py:25
  41.9 3.8 %collective-permute-start.8 = (f32[12,2,256]{2,1,0:T(2,128)S(1)}, f32[12,2,256]{2,1,0:T(2,128)S(1)}, u32[]{:S(2)}, u32[]{:S(2)}) collective-permute-start(f32[12,2,256]{2,1,0:T(2,128)S(1)} %get-tuple-element.6), channel_id=1, source_target_pairs={{0,2},{2,0},{1,3},{3,1},{4,6},{6,4},{5,7},{7,5},{8,10},{10,8},{9,1... | collective-permute-start | bytes 73736 | tf_op jit(solution)/shard_map/ppermute | solution.py:24
  46.1 1.9 %collective-permute-start.10 = (f32[12,68,2]{2,1,0:T(8,128)S(1)}, f32[12,68,2]{2,1,0:T(8,128)S(1)}, u32[]{:S(2)}, u32[]{:S(2)}) collective-permute-start(f32[12,68,2]{2,1,0:T(8,128)S(1)} %get-tuple-element.3), channel_id=1, source_target_pairs={{0,1},{1,0},{2,3},{3,2},{4,5},{5,4},{6,7},{7,6},{8,9},{9,8},{10,11... | collective-permute-start | bytes 19592 | tf_op jit(solution)/shard_map/ppermute | solution.py:24
  46.1 2.4 %collective-permute-start.11 = (f32[12,68,2]{2,1,0:T(8,128)S(1)}, f32[12,68,2]{2,1,0:T(8,128)S(1)}, u32[]{:S(2)}, u32[]{:S(2)}) collective-permute-start(f32[12,68,2]{2,1,0:T(8,128)S(1)} %get-tuple-element.2), channel_id=1, source_target_pairs={{1,0},{0,1},{3,2},{2,3},{5,4},{4,5},{7,6},{6,7},{9,8},{8,9},{11,10... | collective-permute-start | bytes 19592 | tf_op jit(solution)/shard_map/ppermute | solution.py:25
